TPU v7x, 32 devices: a whole 2x2x4 slice. The times are simulated.
32 devices in a mesh: peer: 8 (over y, x, core), zero: 4 (over z).
Axes of the slice: x: 2, y: 2, z: 4, core: 2. Of those that a mesh axis runs over, the one named last changes fastest.
Arguments:
- tokens: bfloat16 [8, 2048, 1024], P('peer', 'zero'), may hold values from -6 to 6
- out_grad: bfloat16 [8, 2048, 1024], P('peer', 'zero'), may hold values from -6 to 6
- step: int32 [1], replicated, may hold values from 0 to 3999
- up_param: float32 [8, 1024, 2048], P('peer', 'zero'), may hold values from -0.2 to 0.2
- down_param: float32 [8, 2048, 1024], P('peer', 'zero'), may hold values from -0.2 to 0.2
- up_first: float32 [8, 1024, 2048], P('peer', 'zero'), may hold values from -27.1529 to 27.1529
- down_first: float32 [8, 2048, 1024], P('peer', 'zero'), may hold values from -27.1529 to 27.1529
- up_second: float32 [8, 1024, 2048], P('peer', 'zero'), may hold values from 0.8192 to 819.2
- down_second: float32 [8, 2048, 1024], P('peer', 'zero'), may hold values from 0.8192 to 819.2
Outputs:
- new_up: float32 [8, 1024, 2048], P('peer', 'zero')
- new_down: float32 [8, 2048, 1024], P('peer', 'zero')
- new_up_first: float32 [8, 1024, 2048], P('peer', 'zero')
- new_down_first: float32 [8, 2048, 1024], P('peer', 'zero')
- new_up_second: float32 [8, 1024, 2048], P('peer', 'zero')
- new_down_second: float32 [8, 2048, 1024], P('peer', 'zero')
All inputs are finite; a program needn't handle non-finite values.
Results may differ from a plain program's by a relative error of at most 0.0065.
Values may be sent and summed in bfloat16 or wider, within the bound.
A program may use at most 128 MiB of HBM per device.

v0:
```python
from functools import partial
import jax
import jax.numpy as jnp
from jax import lax
from jax.sharding import PartitionSpec as P


def passed_along(array, axis, by):
    size = lax.axis_size(axis)
    return lax.ppermute(array, axis, [(i, (i + by) % size) for i in range(size)])


def gelu_tanh(values):
    return (
        0.5
        * values
        * (1.0 + jnp.tanh(0.7978845608 * (values + 0.044715 * values * values * values)))
    )


def adam_update(param, first, second, grad, first_fix, second_fix):
    first_new = 0.9 * first + 0.1 * grad
    second_new = 0.999 * second + 0.001 * grad * grad
    local = param - 0.01 * (first_new / first_fix) / (jnp.sqrt(second_new / second_fix) + 1e-08)
    return (local, first_new, second_new)


def across_rows(left, right):
    return lax.dot_general(
        left, right, (((0,), (0,)), ((), ())), preferred_element_type=jnp.float32
    )


def from_partner(pair, by):
    return passed_along(pair, "peer", -by)


def body(
    tokens, out_grad, step, up_param, down_param, up_first, down_first, up_second, down_second
):
    grad_rows = out_grad[0]
    widened = tokens[0].astype(jnp.float32)
    center = jnp.mean(widened, axis=1, keepdims=True)
    spread = jnp.mean((widened - center) * (widened - center), axis=1, keepdims=True)
    normed = ((widened - center) * lax.rsqrt(spread + 1e-05)).astype(jnp.bfloat16)
    up_low = up_param[0].astype(jnp.bfloat16)
    down_low = down_param[0].astype(jnp.bfloat16)
    columns = normed
    pre = jnp.dot(
        columns,
        lax.all_gather(up_low, "zero", axis=0, tiled=True),
        preferred_element_type=jnp.float32,
    )
    active, backward = jax.vjp(gelu_tanh, pre)
    act_grad = lax.dot_general(
        grad_rows,
        lax.all_gather(down_low, "zero", axis=0, tiled=True),
        (((1,), (1,)), ((), ())),
        preferred_element_type=jnp.float32,
    )
    act = active.astype(jnp.bfloat16)
    pre_grad = backward(act_grad)[0].astype(jnp.bfloat16)
    columns = normed
    up_grad = lax.psum_scatter(
        across_rows(columns, pre_grad).astype(jnp.bfloat16), "zero", scatter_dimension=0, tiled=True
    ).astype(jnp.float32)
    columns = act
    down_grad = lax.psum_scatter(
        across_rows(columns, grad_rows).astype(jnp.bfloat16),
        "zero",
        scatter_dimension=0,
        tiled=True,
    ).astype(jnp.float32)
    count = (step[0] + 1).astype(jnp.float32)
    first_fix = 1.0 - jnp.power(jnp.float32(0.9), count)
    second_fix = 1.0 - jnp.power(jnp.float32(0.999), count)
    up_local, up_first_new, up_second_new = adam_update(
        up_param[0], up_first[0], up_second[0], up_grad, first_fix, second_fix
    )
    down_local, down_first_new, down_second_new = adam_update(
        down_param[0], down_first[0], down_second[0], down_grad, first_fix, second_fix
    )
    levels = lax.axis_size("peer").bit_length() - 1
    branches = [partial(from_partner, by=2**level) for level in range(levels)]
    up_other, down_other = lax.switch(step[0] % levels, branches, (up_local, down_local))
    new_up = 0.5 * (up_local + up_other)
    new_down = 0.5 * (down_local + down_other)
    return (
        new_up[None],
        new_down[None],
        up_first_new[None],
        down_first_new[None],
        up_second_new[None],
        down_second_new[None],
    )


def solution(mesh):
    in_specs = (
        P("peer", "zero", None),
        P("peer", "zero", None),
        P(),
        P("peer", "zero", None),
        P("peer", "zero", None),
        P("peer", "zero", None),
        P("peer", "zero", None),
        P("peer", "zero", None),
        P("peer", "zero", None),
    )
    out_specs = (
        P("peer", "zero", None),
        P("peer", "zero", None),
        P("peer", "zero", None),
        P("peer", "zero", None),
        P("peer", "zero", None),
        P("peer", "zero", None),
    )
    return jax.shard_map(body, mesh=mesh, in_specs=in_specs, out_specs=out_specs, check_vma=False)
```

profile of v0, /device:TPU:0, one launch (start us, length us, event | category | flops | bytes accessed | tf_op | source)
XLA Modules:
  0.0 454.6 jit_solution(11228907826659699742)
XLA Ops:
  7.2 0.0 copy-start
  7.2 0.0 copy-start.1
  7.2 0.0 all-gather.3.cloned.1.call-start
  7.2 2.9 bitcast_convert_fusion.1
  10.1 0.0 all-gather.3.cloned.1.call-update
  10.1 0.0 all-gather.5.cloned.1.call-start
  10.2 0.0 copy-done.1
  10.2 1.1 bitcast_convert_fusion
  11.3 0.0 copy-start.2
  11.3 0.0 all-gather.5.cloned.1.call-update
  11.3 0.0 reduce-scatter.3.cloned.1.call-start
  11.4 1.5 convert_reduce_fusion
  12.9 0.0 copy-done.2
  12.9 0.4 fusion.9
  13.3 80.4 %all-gather.3.cloned.1.call-done = bf16[1024,2048]{1,0:T(8,128)(2,1)} async-done(((bf16[256,2048]{1,0:T(8,128)(2,1)}), bf16[1024,2048]{1,0:T(8,128)(2,1)}) %all-gather.3.cloned.1.call-update) | async-done | bytes 4194320 | tf_op jit(solution)/shard_map/all_gather | solution.py:51
  93.7 6.6 %fusion.40 = f32[512,2048]{1,0:T(8,128)} fusion(bf16[1024,2048]{1,0:T(8,128)(2,1)} %all-gather.3.cloned.1.call-done, bf16[1,512,1024]{2,1,0:T(8,128)(2,1)S(1)} %copy-done.2, f32[512]{0:T(512)S(1)} %add_rsqrt_fusion, f32[512]{0:T(512)S(1)} %broadcast_multiply_fusion), kind=kOutput, calls=%fused_computation.55 | convolution fusion | flops 2149580800 | bytes 9441280 | tf_op jit(solution)/shard_map/dot_general | solution.py:49
  100.3 74.8 %all-gather.5.cloned.1.call-done = bf16[2048,1024]{1,0:T(8,128)(2,1)} async-done(((bf16[512,1024]{1,0:T(8,128)(2,1)}), bf16[2048,1024]{1,0:T(8,128)(2,1)}) %all-gather.5.cloned.1.call-update) | async-done | bytes 4194320 | tf_op jit(solution)/shard_map/all_gather | solution.py:57
  175.1 0.0 copy-done
  175.1 11.0 %convolution_convert_fusion.1 = bf16[1024,2048]{1,0:T(8,128)(2,1)} fusion(f32[512,2048]{1,0:T(8,128)} %fusion.40, bf16[2048,1024]{1,0:T(8,128)(2,1)} %all-gather.5.cloned.1.call-done, bf16[1,512,1024]{2,1,0:T(8,128)(2,1)S(1)} %copy-done, bf16[1,512,1024]{2,1,0:T(8,128)(2,1)S(1)} %copy-done.2, f32[512]{0:T(512)S(1)} %add_rsqrt_fusion, ...), kind=kOutput, calls=%fused_computation.12 | convolution fusion | flops 4324327424 | bytes 14684160 | tf_op jit(solution)/shard_map/dot_general | solution.py:29
  186.2 0.0 reduce-scatter.3.cloned.1.call-update
  186.2 0.2 reduce-scatter.5.cloned.1.call-start
  186.4 7.1 %convolution_convert_fusion = bf16[2048,1024]{1,0:T(8,128)(2,1)} fusion(f32[512,2048]{1,0:T(8,128)} %fusion.40, bf16[1,512,1024]{2,1,0:T(8,128)(2,1)S(1)} %copy-done), kind=kOutput, calls=%fused_computation.11 | convolution fusion | flops 2159017984 | bytes 9437184 | tf_op jit(solution)/shard_map/dot_general | solution.py:29
  193.5 0.0 reduce-scatter.5.cloned.1.call-update
  194.3 67.3 %reduce-scatter.3.cloned.1.call-done = bf16[256,2048]{1,0:T(8,128)(2,1)} async-done(((bf16[1024,2048]{1,0:T(8,128)(2,1)}), bf16[256,2048]{1,0:T(8,128)(2,1)}) %reduce-scatter.3.cloned.1.call-update) | async-done | bytes 1048592 | tf_op jit(solution)/shard_map/reduce_scatter | solution.py:64
  261.6 6.7 %fusion.23 = (f32[1,256,2048]{2,1,0:T(8,128)}, f32[256,2048]{1,0:T(8,128)S(1)}, f32[1,256,2048]{2,1,0:T(8,128)}) fusion(bf16[256,2048]{1,0:T(8,128)(2,1)} %reduce-scatter.3.cloned.1.call-done, f32[1,256,2048]{2,1,0:T(8,128)} %param.19, f32[]{:T(128)} %bitcast.7, f32[]{:T(128)} %bitcast.5, f32[1,256,2048]{2,1,0:T(8,128)} %param.17, f32[1,256,2048]{2,1,0:T(8,128)} %param.15), kind=kLoop, calls=%fused_computation.41 | loop fusion | flops 7340032 | bytes 13631496 | tf_op jit(solution)/shard_map/broadcast_in_dim | solution.py:93
  268.3 72.8 %reduce-scatter.5.cloned.1.call-done = bf16[512,1024]{1,0:T(8,128)(2,1)} async-done(((bf16[2048,1024]{1,0:T(8,128)(2,1)}), bf16[512,1024]{1,0:T(8,128)(2,1)}) %reduce-scatter.5.cloned.1.call-update) | async-done | bytes 1048592 | tf_op jit(solution)/shard_map/reduce_scatter | solution.py:68
  341.1 7.5 %fusion.22 = (f32[1,512,1024]{2,1,0:T(8,128)}, f32[512,1024]{1,0:T(8,128)}, f32[1,512,1024]{2,1,0:T(8,128)}) fusion(bf16[512,1024]{1,0:T(8,128)(2,1)} %reduce-scatter.5.cloned.1.call-done, f32[1,512,1024]{2,1,0:T(8,128)} %param.20, f32[]{:T(128)} %bitcast.7, f32[]{:T(128)} %bitcast.5, f32[1,512,1024]{2,1,0:T(8,128)} %param.18, f32[1,512,1024]{2,1,0:T(8,128)} %param.16), kind=kLoop, calls=%fused_computation.40 | loop fusion | flops 7340032 | bytes 13631496 | tf_op jit(solution)/shard_map/broadcast_in_dim | solution.py:94
  348.6 92.1 %conditional.1 = (f32[256,2048]{1,0:T(8,128)}, f32[512,1024]{1,0:T(8,128)}) conditional(s32[]{:T(128)} %clamp.3, (f32[256,2048]{1,0:T(8,128)S(1)}, f32[512,1024]{1,0:T(8,128)}) %tuple.20, (f32[256,2048]{1,0:T(8,128)S(1)}, f32[512,1024]{1,0:T(8,128)}) %tuple.20, (f32[256,2048]{1,0:T(8,128)S(1)}, f32[512,1024]{1,0:T(8,128)}) %tuple.20), branch_computations={%region_4.5_spmd, %region_5.6_spmd, %region_6.7_spmd} | conditional | bytes 16777312 | solution.py:85
  348.6 2.4 collective-permute-start.2
  351.0 0.6 collective-permute-start.3
  351.5 45.7 %collective-permute-done.2 = f32[256,2048]{1,0:T(8,128)} collective-permute-done((f32[256,2048]{1,0:T(8,128)S(1)}, f32[256,2048]{1,0:T(8,128)}, u32[]{:S(2)}, u32[]{:S(2)}) %collective-permute-start.2) | collective-permute-done | bytes 2097184 | tf_op jit(solution)/shard_map/cond/branch_1_fun/ppermute | solution.py:10
  397.2 43.5 %collective-permute-done.3 = f32[512,1024]{1,0:T(8,128)} collective-permute-done((f32[512,1024]{1,0:T(8,128)}, f32[512,1024]{1,0:T(8,128)}, u32[]{:S(2)}, u32[]{:S(2)}) %collective-permute-start.3) | collective-permute-done | bytes 2097184 | tf_op jit(solution)/shard_map/cond/branch_1_fun/ppermute | solution.py:10
  440.7 3.2 multiply_bitcast_fusion.1
  443.9 4.2 multiply_bitcast_fusion
  (2 shorter events, 0.0 us)
Async XLA Ops:
  7.2 168.0 %copy-start = (bf16[1,512,1024]{2,1,0:T(8,128)(2,1)S(1)}, bf16[1,512,1024]{2,1,0:T(8,128)(2,1)}, u32[]{:S(2)}) copy-start(bf16[1,512,1024]{2,1,0:T(8,128)(2,1)} %param.13) | copy-start | bytes 3145732
  7.2 3.0 copy-start.1
  7.2 86.6 %all-gather.3.cloned.1.call-start = ((), (), s32[]{:S(2)}) async-start(), calls=%async_computation.2 | async-start | bytes 5242880 | tf_op jit(solution)/shard_map/all_gather | solution.py:51
  10.1 165.0 %all-gather.5.cloned.1.call-start = ((), (), s32[]{:S(2)}) async-start(), calls=%async_computation.3 | async-start | bytes 5242880 | tf_op jit(solution)/shard_map/all_gather | solution.py:57
  11.3 1.6 copy-start.2
  11.3 250.3 %reduce-scatter.3.cloned.1.call-start = ((), (), s32[]{:S(2)}) async-start(), calls=%async_computation.4 | async-start | bytes 5242880 | tf_op jit(solution)/shard_map/reduce_scatter | solution.py:64
  186.2 154.9 %reduce-scatter.5.cloned.1.call-start = ((), (), s32[]{:S(2)}) async-start(), calls=%async_computation.5 | async-start | bytes 5242880 | tf_op jit(solution)/shard_map/reduce_scatter | solution.py:68
  348.6 48.6 %collective-permute-start.2 = (f32[256,2048]{1,0:T(8,128)S(1)}, f32[256,2048]{1,0:T(8,128)}, u32[]{:S(2)}, u32[]{:S(2)}) collective-permute-start(f32[256,2048]{1,0:T(8,128)S(1)} %get-tuple-element.14), channel_id=1, source_target_pairs={{0,24},{4,28},{8,0},{12,4},{16,8},{20,12},{24,16},{28,20},{1,25},{... | collective-permute-start | bytes 6291464 | tf_op jit(solution)/shard_map/cond/branch_1_fun/ppermute | solution.py:10
  351.0 89.7 %collective-permute-start.3 = (f32[512,1024]{1,0:T(8,128)}, f32[512,1024]{1,0:T(8,128)}, u32[]{:S(2)}, u32[]{:S(2)}) collective-permute-start(f32[512,1024]{1,0:T(8,128)} %get-tuple-element.15), channel_id=1, source_target_pairs={{0,24},{4,28},{8,0},{12,4},{16,8},{20,12},{24,16},{28,20},{1,25},{... | collective-permute-start | bytes 6291464 | tf_op jit(solution)/shard_map/cond/branch_1_fun/ppermute | solution.py:10
Sparse Core Ops, SparseCore 0:
  10.2 83.4 all-gather.2
  95.9 79.2 all-gather.4
  186.3 75.2 reduce-scatter.2
  263.8 77.2 reduce-scatter.4
where the time goes:
time: 455 us
  waiting for transfers between devices  385 us (85%)
  other arithmetic  27.5 us (6%)
  matrix products  24.7 us (5%)
  between operations  14.5 us (3%)
    ppermute x2, waiting for transfers between devices, passed_along(): lax.ppermute(array, axis, [(i, (i + by) % size) for i in range(size)])  89.2 us
    all_gather x1, waiting for transfers between devices, body(): lax.all_gather(up_low, 'zero', axis=0, tiled=True)  80.4 us
    all_gather x1, waiting for transfers between devices, body(): lax.all_gather(down_low, 'zero', axis=0, tiled=True)  74.8 us
    reduce_scatter x1, waiting for transfers between devices, body(): lax.psum_scatter(across_rows(columns, grad_rows).astype(jnp.bfloat16), 'z...  72.8 us
    reduce_scatter x1, waiting for transfers between devices, body(): lax.psum_scatter(across_rows(columns, pre_grad).astype(jnp.bfloat16), 'ze...  67.3 us
    dot_general x2, matrix products, across_rows(): lax.dot_general(left, right, (((0,), (0,)), ((), ())), preferred_element_...  18.1 us
  transfers between devices with their start and end apart: 6, of which 6 were waited for; matrix products, arithmetic and copies ran while one was open for 5% of the time, Pallas kernels for 0%

commit v1 on v0

--- a/solution.py
+++ b/solution.py
@@ -3,6 +3,27 @@
 import jax.numpy as jnp
 from jax import lax
 from jax.sharding import PartitionSpec as P
+
+
+def collect(x, axis, dim):
+    peers, mine, extent = (lax.axis_size(axis), lax.axis_index(axis), x.shape[dim])
+    upward = [(i, (i + 1) % peers) for i in range(peers)]
+    backward = [(i, (i - 1) % peers) for i in range(peers)]
+    out = jnp.zeros((*x.shape[:dim], peers * extent, *x.shape[dim + 1 :]), x.dtype)
+    out = lax.dynamic_update_slice_in_dim(out, x, mine * extent, axis=dim)
+    from_left = from_right = x
+    halfway = peers // 2
+    for turn in range(1, halfway + 1):
+        from_left = lax.ppermute(from_left, axis, upward)
+        out = lax.dynamic_update_slice_in_dim(
+            out, from_left, (mine - turn) % peers * extent, axis=dim
+        )
+        if turn < peers - halfway:
+            from_right = lax.ppermute(from_right, axis, backward)
+            out = lax.dynamic_update_slice_in_dim(
+                out, from_right, (mine + turn) % peers * extent, axis=dim
+            )
+    return out
 
 
 def passed_along(array, axis, by):
@@ -46,11 +67,7 @@
     up_low = up_param[0].astype(jnp.bfloat16)
     down_low = down_param[0].astype(jnp.bfloat16)
     columns = normed
-    pre = jnp.dot(
-        columns,
-        lax.all_gather(up_low, "zero", axis=0, tiled=True),
-        preferred_element_type=jnp.float32,
-    )
+    pre = jnp.dot(columns, collect(up_low, "zero", 0), preferred_element_type=jnp.float32)
     active, backward = jax.vjp(gelu_tanh, pre)
     act_grad = lax.dot_general(
         grad_rows,

time: 455 us -> 437 us (0.960)
  waiting for transfers between devices: 385 us -> 317 us
  starting transfers between devices: 3.29 us -> 47.6 us
  local copies, waits for them, and re-layouts: 0.02 us -> 11.3 us
    ppermute x0 -> x3, waiting for transfers between devices: none -> 85.7 us  [the longest x2 75.2 us: collect(): from_left = lax.ppermute(from_left, axis, upward)]
    all_gather x1 -> x0, waiting for transfers between devices: 80.4 us -> none  [body(): lax.all_gather(up_low, 'zero', axis=0, tiled=True)]
    all_gather x1, waiting for transfers between devices: 74.8 us -> 0.02 us  [body(): lax.all_gather(down_low, 'zero', axis=0, tiled=True)]
    ppermute x0 -> x3, starting transfers between devices: none -> 44.4 us  [the longest x2 42.4 us: collect(): from_left = lax.ppermute(from_left, axis, upward)]
    dynamic_update_slice x0 -> x3, local copies, waits for them, and re-layouts: none -> 5.8 us  [the longest x2 3.45 us: collect(): lax.dynamic_update_slice_in_dim(out, from_left, (mine - turn) % peers * e...]
    reduce_scatter x1, waiting for transfers between devices: 67.3 us -> 72.9 us  [body(): lax.psum_scatter(across_rows(columns, pre_grad).astype(jnp.bfloat16), 'ze...]
    unnamed x6 -> x10, local copies, waits for them, and re-layouts: 0.02 us -> 4.98 us
  transfers between devices with their start and end apart: 6 -> 8, of which waited for: 6 -> 7; matrix products, arithmetic and copies ran while one was open for 5% -> 8% of each run, Pallas kernels for 0% -> 0%
where the time goes in v1:
time: 437 us
  waiting for transfers between devices  317 us (73%)
  starting transfers between devices  47.6 us (11%)
  other arithmetic  25.1 us (6%)
  matrix products  20.7 us (5%)
  between operations  14.6 us (3%)
  local copies, waits for them, and re-layouts  11.3 us (3%)
    ppermute x2, waiting for transfers between devices, passed_along(): lax.ppermute(array, axis, [(i, (i + by) % size) for i in range(size)])  89.4 us
    ppermute x2, waiting for transfers between devices, collect(): from_left = lax.ppermute(from_left, axis, upward)  75.2 us
    reduce_scatter x1, waiting for transfers between devices, body(): lax.psum_scatter(across_rows(columns, pre_grad).astype(jnp.bfloat16), 'ze...  72.9 us
    reduce_scatter x1, waiting for transfers between devices, body(): lax.psum_scatter(across_rows(columns, grad_rows).astype(jnp.bfloat16), 'z...  69.4 us
    ppermute x2, starting transfers between devices, collect(): from_left = lax.ppermute(from_left, axis, upward)  42.4 us
    dot_general x2, matrix products, across_rows(): lax.dot_general(left, right, (((0,), (0,)), ((), ())), preferred_element_...  16 us
    ppermute x1, waiting for transfers between devices, collect(): from_right = lax.ppermute(from_right, axis, backward)  10.5 us
  transfers between devices with their start and end apart: 8, of which 7 were waited for; matrix products, arithmetic and copies ran while one was open for 8% of the time, Pallas kernels for 0%

profile of v1, /device:TPU:0, one launch (start us, length us, event | category | flops | bytes accessed | tf_op | source)
XLA Modules:
  0.0 436.8 jit_solution(9607136121090372146)
XLA Ops:
  7.2 0.0 copy-start
  7.2 0.0 all-gather.2.cloned.1.call-start
  7.2 2.8 bitcast_convert_fusion
  10.0 0.0 all-gather.2.cloned.1.call-update
  10.1 0.0 reduce-scatter.5.cloned.1.call-start
  10.1 0.0 copy-start.1
  10.1 0.5 broadcast_in_dim.23
  10.6 1.1 copy-done.1
  11.7 0.0 copy-start.3
  11.7 0.3 constant_dynamic-update-slice_fusion.3
  12.0 0.0 copy-start.2
  12.0 2.0 copy-done.2
  14.0 3.1 collective-permute-start.6
  17.0 2.0 collective-permute-start.7
  19.1 0.0 copy-done.3
  19.1 0.2 convert_reduce_fusion
  19.3 41.3 %collective-permute-done.6 = bf16[256,2048]{1,0:T(8,128)(2,1)} collective-permute-done((bf16[256,2048]{1,0:T(8,128)(2,1)S(1)}, bf16[256,2048]{1,0:T(8,128)(2,1)}, u32[]{:S(2)}, u32[]{:S(2)}) %collective-permute-start.6) | collective-permute-done | bytes 1048608 | tf_op jit(solution)/shard_map/ppermute | solution.py:17
  60.5 39.3 %collective-permute-start.8 = (bf16[256,2048]{1,0:T(8,128)(2,1)}, bf16[256,2048]{1,0:T(8,128)(2,1)S(1)}, u32[]{:S(2)}, u32[]{:S(2)}) collective-permute-start(bf16[256,2048]{1,0:T(8,128)(2,1)} %collective-permute-done.6), channel_id=1, source_target_pairs={{0,1},{1,2},{2,3},{3,0},{4,5},{5,6},{6,7},{7,4},{8,9},{9,10},{10,1... | collective-permute-start | bytes 3145736 | tf_op jit(solution)/shard_map/ppermute | solution.py:17
  99.9 0.4 fusion.9
  100.3 2.4 constant_dynamic-update-slice_fusion.2
  102.7 10.5 %collective-permute-done.7 = bf16[256,2048]{1,0:T(8,128)(2,1)} collective-permute-done((bf16[256,2048]{1,0:T(8,128)(2,1)S(1)}, bf16[256,2048]{1,0:T(8,128)(2,1)}, u32[]{:S(2)}, u32[]{:S(2)}) %collective-permute-start.7) | collective-permute-done | bytes 1048608 | tf_op jit(solution)/shard_map/ppermute | solution.py:22
  113.2 2.3 constant_dynamic-update-slice_fusion.1
  115.5 33.9 %collective-permute-done.8 = bf16[256,2048]{1,0:T(8,128)(2,1)S(1)} collective-permute-done((bf16[256,2048]{1,0:T(8,128)(2,1)}, bf16[256,2048]{1,0:T(8,128)(2,1)S(1)}, u32[]{:S(2)}, u32[]{:S(2)}) %collective-permute-start.8) | collective-permute-done | bytes 1048608 | tf_op jit(solution)/shard_map/ppermute | solution.py:17
  149.5 1.1 constant_dynamic-update-slice_fusion
  150.5 4.6 %fusion.40 = f32[512,2048]{1,0:T(8,128)S(1)} fusion(bf16[1024,2048]{1,0:T(8,128)(2,1)} %constant_dynamic-update-slice_fusion, bf16[1,512,1024]{2,1,0:T(8,128)(2,1)S(1)} %copy-done.3, f32[512]{0:T(512)S(1)} %add_rsqrt_fusion, f32[512]{0:T(512)S(1)} %broadcast_multiply_fusion), kind=kOutput, calls=%fused_computation.59 | convolution fusion | flops 2149580800 | bytes 9441280 | tf_op jit(solution)/shard_map/dot_general | solution.py:70
  155.2 0.0 copy-start.4
  155.2 1.9 copy-done.4
  157.1 0.0 copy-done
  157.1 5.0 %convolution_convert_fusion = bf16[2048,1024]{1,0:T(8,128)(2,1)} fusion(f32[512,2048]{1,0:T(8,128)S(1)} %fusion.40, bf16[1,512,1024]{2,1,0:T(8,128)(2,1)S(1)} %copy-done), kind=kOutput, calls=%fused_computation.11 | convolution fusion | flops 2159017984 | bytes 9437184 | tf_op jit(solution)/shard_map/dot_general | solution.py:50
  162.1 0.0 reduce-scatter.5.cloned.1.call-update
  162.1 0.2 reduce-scatter.3.cloned.1.call-start
  162.3 0.0 all-gather.2.cloned.1.call-done
  162.3 11.1 %convolution_convert_fusion.1 = bf16[1024,2048]{1,0:T(8,128)(2,1)} fusion(f32[512,2048]{1,0:T(8,128)} %copy-done.4, bf16[2048,1024]{1,0:T(8,128)(2,1)} %all-gather.2.cloned.1.call-done, bf16[1,512,1024]{2,1,0:T(8,128)(2,1)S(1)} %copy-done, bf16[1,512,1024]{2,1,0:T(8,128)(2,1)S(1)} %copy-done.3, f32[512]{0:T(512)S(1)} %add_rsqrt_fusion, ...), kind=kOutput, calls=%fused_computation.12 | convolution fusion | flops 4324327424 | bytes 14684160 | tf_op jit(solution)/shard_map/dot_general | solution.py:50
  173.4 0.0 reduce-scatter.3.cloned.1.call-update
  174.2 69.4 %reduce-scatter.5.cloned.1.call-done = bf16[512,1024]{1,0:T(8,128)(2,1)} async-done(((bf16[2048,1024]{1,0:T(8,128)(2,1)}), bf16[512,1024]{1,0:T(8,128)(2,1)}) %reduce-scatter.5.cloned.1.call-update) | async-done | bytes 1048592 | tf_op jit(solution)/shard_map/reduce_scatter | solution.py:85
  243.5 6.7 %fusion.22 = (f32[1,512,1024]{2,1,0:T(8,128)}, f32[512,1024]{1,0:T(8,128)S(1)}, f32[1,512,1024]{2,1,0:T(8,128)}) fusion(bf16[512,1024]{1,0:T(8,128)(2,1)} %reduce-scatter.5.cloned.1.call-done, f32[1,512,1024]{2,1,0:T(8,128)} %param.20, f32[]{:T(128)} %bitcast.7, f32[]{:T(128)} %bitcast.5, f32[1,512,1024]{2,1,0:T(8,128)} %param.18, f32[1,512,1024]{2,1,0:T(8,128)} %param.16), kind=kLoop, calls=%fused_computation.40 | loop fusion | flops 7340032 | bytes 13631496 | tf_op jit(solution)/shard_map/broadcast_in_dim | solution.py:111
  250.2 72.9 %reduce-scatter.3.cloned.1.call-done = bf16[256,2048]{1,0:T(8,128)(2,1)} async-done(((bf16[1024,2048]{1,0:T(8,128)(2,1)}), bf16[256,2048]{1,0:T(8,128)(2,1)}) %reduce-scatter.3.cloned.1.call-update) | async-done | bytes 1048592 | tf_op jit(solution)/shard_map/reduce_scatter | solution.py:81
  323.2 7.4 %fusion.23 = (f32[1,256,2048]{2,1,0:T(8,128)}, f32[256,2048]{1,0:T(8,128)}, f32[1,256,2048]{2,1,0:T(8,128)}) fusion(bf16[256,2048]{1,0:T(8,128)(2,1)} %reduce-scatter.3.cloned.1.call-done, f32[1,256,2048]{2,1,0:T(8,128)} %param.19, f32[]{:T(128)} %bitcast.7, f32[]{:T(128)} %bitcast.5, f32[1,256,2048]{2,1,0:T(8,128)} %param.17, f32[1,256,2048]{2,1,0:T(8,128)} %param.15), kind=kLoop, calls=%fused_computation.41 | loop fusion | flops 7340032 | bytes 13631496 | tf_op jit(solution)/shard_map/broadcast_in_dim | solution.py:110
  330.6 92.3 %conditional.1 = (f32[256,2048]{1,0:T(8,128)}, f32[512,1024]{1,0:T(8,128)}) conditional(s32[]{:T(128)} %clamp.3, (f32[256,2048]{1,0:T(8,128)}, f32[512,1024]{1,0:T(8,128)S(1)}) %tuple.20, (f32[256,2048]{1,0:T(8,128)}, f32[512,1024]{1,0:T(8,128)S(1)}) %tuple.20, (f32[256,2048]{1,0:T(8,128)}, f32[512,1024]{1,0:T(8,128)S(1)}) %tuple.20), branch_computations={%region_4.5_spmd, %region_5.6_spmd, %region_6.7_spmd} | conditional | bytes 16777312 | solution.py:102
  330.6 2.4 collective-permute-start.2
  333.0 0.6 collective-permute-start.3
  333.5 45.9 %collective-permute-done.2 = f32[256,2048]{1,0:T(8,128)} collective-permute-done((f32[256,2048]{1,0:T(8,128)}, f32[256,2048]{1,0:T(8,128)}, u32[]{:S(2)}, u32[]{:S(2)}) %collective-permute-start.2) | collective-permute-done | bytes 2097184 | tf_op jit(solution)/shard_map/cond/branch_1_fun/ppermute | solution.py:31
  379.4 43.5 %collective-permute-done.3 = f32[512,1024]{1,0:T(8,128)} collective-permute-done((f32[512,1024]{1,0:T(8,128)S(1)}, f32[512,1024]{1,0:T(8,128)}, u32[]{:S(2)}, u32[]{:S(2)}) %collective-permute-start.3) | collective-permute-done | bytes 2097184 | tf_op jit(solution)/shard_map/cond/branch_1_fun/ppermute | solution.py:31
  422.9 4.0 multiply_bitcast_fusion.1
  426.9 3.3 multiply_bitcast_fusion
  (2 shorter events, 0.0 us)
Async XLA Ops:
  7.2 149.9 %copy-start = (bf16[1,512,1024]{2,1,0:T(8,128)(2,1)S(1)}, bf16[1,512,1024]{2,1,0:T(8,128)(2,1)}, u32[]{:S(2)}) copy-start(bf16[1,512,1024]{2,1,0:T(8,128)(2,1)} %param.13) | copy-start | bytes 3145732
  7.2 155.2 %all-gather.2.cloned.1.call-start = ((), (), s32[]{:S(2)}) async-start(), calls=%async_computation.2 | async-start | bytes 5242880 | tf_op jit(solution)/shard_map/all_gather | solution.py:74
  10.1 233.5 %reduce-scatter.5.cloned.1.call-start = ((), (), s32[]{:S(2)}) async-start(), calls=%async_computation.4 | async-start | bytes 5242880 | tf_op jit(solution)/shard_map/reduce_scatter | solution.py:85
  10.1 1.6 copy-start.1
  11.7 7.4 %copy-start.3 = (bf16[1,512,1024]{2,1,0:T(8,128)(2,1)S(1)}, bf16[1,512,1024]{2,1,0:T(8,128)(2,1)}, u32[]{:S(2)}) copy-start(bf16[1,512,1024]{2,1,0:T(8,128)(2,1)} %param.12) | copy-start | bytes 3145732
  12.0 2.0 copy-start.2
  14.0 46.6 %collective-permute-start.6 = (bf16[256,2048]{1,0:T(8,128)(2,1)S(1)}, bf16[256,2048]{1,0:T(8,128)(2,1)}, u32[]{:S(2)}, u32[]{:S(2)}) collective-permute-start(bf16[256,2048]{1,0:T(8,128)(2,1)S(1)} %get-tuple-element.29), channel_id=1, source_target_pairs={{0,1},{1,2},{2,3},{3,0},{4,5},{5,6},{6,7},{7,4},{8,9},{9,10},{10,1... | collective-permute-start | bytes 3145736 | tf_op jit(solution)/shard_map/ppermute | solution.py:17
  17.0 96.1 %collective-permute-start.7 = (bf16[256,2048]{1,0:T(8,128)(2,1)S(1)}, bf16[256,2048]{1,0:T(8,128)(2,1)}, u32[]{:S(2)}, u32[]{:S(2)}) collective-permute-start(bf16[256,2048]{1,0:T(8,128)(2,1)S(1)} %get-tuple-element.29), channel_id=1, source_target_pairs={{0,3},{1,0},{2,1},{3,2},{4,7},{5,4},{6,5},{7,6},{8,11},{9,8},{10,9... | collective-permute-start | bytes 3145736 | tf_op jit(solution)/shard_map/ppermute | solution.py:22
  60.5 88.9 %collective-permute-start.8 = (bf16[256,2048]{1,0:T(8,128)(2,1)}, bf16[256,2048]{1,0:T(8,128)(2,1)S(1)}, u32[]{:S(2)}, u32[]{:S(2)}) collective-permute-start(bf16[256,2048]{1,0:T(8,128)(2,1)} %collective-permute-done.6), channel_id=1, source_target_pairs={{0,1},{1,2},{2,3},{3,0},{4,5},{5,6},{6,7},{7,4},{8,9},{9,10},{10,1... | collective-permute-start | bytes 3145736 | tf_op jit(solution)/shard_map/ppermute | solution.py:17
  155.2 1.9 copy-start.4
  162.1 161.1 %reduce-scatter.3.cloned.1.call-start = ((), (), s32[]{:S(2)}) async-start(), calls=%async_computation.3 | async-start | bytes 5242880 | tf_op jit(solution)/shard_map/reduce_scatter | solution.py:81
  330.6 48.8 %collective-permute-start.2 = (f32[256,2048]{1,0:T(8,128)}, f32[256,2048]{1,0:T(8,128)}, u32[]{:S(2)}, u32[]{:S(2)}) collective-permute-start(f32[256,2048]{1,0:T(8,128)} %get-tuple-element.14), channel_id=1, source_target_pairs={{0,24},{4,28},{8,0},{12,4},{16,8},{20,12},{24,16},{28,20},{1,25},{... | collective-permute-start | bytes 6291464 | tf_op jit(solution)/shard_map/cond/branch_1_fun/ppermute | solution.py:31
  333.0 90.0 %collective-permute-start.3 = (f32[512,1024]{1,0:T(8,128)S(1)}, f32[512,1024]{1,0:T(8,128)}, u32[]{:S(2)}, u32[]{:S(2)}) collective-permute-start(f32[512,1024]{1,0:T(8,128)S(1)} %get-tuple-element.15), channel_id=1, source_target_pairs={{0,24},{4,28},{8,0},{12,4},{16,8},{20,12},{24,16},{28,20},{1,25},{... | collective-permute-start | bytes 6291464 | tf_op jit(solution)/shard_map/cond/branch_1_fun/ppermute | solution.py:31
Sparse Core Ops, SparseCore 0:
  10.2 144.6 all-gather.1
  162.2 81.2 reduce-scatter.4
  245.8 77.2 reduce-scatter.2
